TPU v7x, 32 devices: a whole 2x2x4 slice. The times are simulated.
32 devices in a mesh: depth: 16 (over z, y, x), spec: 2 (over core).
Axes of the slice: x: 2, y: 2, z: 4, core: 2. Of those that a mesh axis runs over, the one named last changes fastest.
Arguments:
- emission: bfloat16 [512, 64, 2048], P('depth', 'spec'), may hold values from 0.099609375 to 2
- opacity: bfloat16 [512, 64, 2048], P('depth', 'spec'), may hold values from 0.29882812 to 3
- bin_extinction: float32 [64], P('spec'), may hold values from 0.1 to 30
- entry: int32 [2048], replicated, may hold values from 0 to 127
- exit_cell: int32 [2048], replicated, may hold values from 384 to 512
- response: float32 [3, 64], P(None, 'spec'), may hold values from 0.05 to 1
Outputs:
- nearer_slab_rgb: float32 [16, 3, 2048], P('depth')
- image: float32 [3, 2048], replicated
All inputs are finite; a program needn't handle non-finite values.
Results may differ from a plain program's by a relative error of at most 0.0003.
Values sent between devices are 32-bit elements; how exact they have to be, the bound alone decides.
A program may use at most 64 MiB of HBM per device.

v0:
```python
import jax
import jax.numpy as jnp
from jax import lax
from jax.sharding import PartitionSpec as P


def merge_slabs(earlier, later):
    return (earlier[0] + earlier[1] * later[0], earlier[1] * later[1])


def body(emission, opacity, bin_extinction, entry, exit_cell, response):
    cells = emission.shape[0]
    sections = lax.axis_size("depth")
    cell_step = 1.0 / (cells * sections)
    depth = lax.axis_index("depth") * cells + jnp.arange(cells, dtype=jnp.int32)
    inside = (depth[:, None] >= entry[None, :]) & (depth[:, None] < exit_cell[None, :])
    live = jnp.where(inside, 1.0, 0.0).astype(jnp.float32)
    tau = bin_extinction[None, :, None] * opacity.astype(jnp.float32) * live[:, None, :] * cell_step
    rows = jnp.arange(cells, dtype=jnp.int32)
    lower = jnp.where(rows[None, :] < rows[:, None], 1.0, 0.0).astype(jnp.float32)
    before = jnp.einsum("ij,jbr->ibr", lower, tau, precision=lax.Precision.HIGHEST)
    light = jnp.sum(
        emission.astype(jnp.float32) * live[:, None, :] * cell_step * jnp.exp(-before), axis=0
    )
    trans = jnp.exp(-jnp.sum(tau, axis=0))
    pieces = (
        lax.all_to_all(light[None], "depth", split_axis=2, concat_axis=0, tiled=True),
        lax.all_to_all(trans[None], "depth", split_axis=2, concat_axis=0, tiled=True),
    )
    totals = lax.associative_scan(merge_slabs, (pieces[0], pieces[1]), axis=0)
    lead_light = jnp.concatenate([jnp.zeros_like(pieces[0][:1]), totals[0][:-1]], axis=0)
    lead_trans = jnp.concatenate([jnp.ones_like(pieces[1][:1]), totals[1][:-1]], axis=0)
    moved_light = lax.all_to_all(lead_light, "depth", split_axis=0, concat_axis=2, tiled=True)
    moved_trans = lax.all_to_all(lead_trans, "depth", split_axis=0, concat_axis=2, tiled=True)
    nearer_radiance = moved_light[0]
    nearer_transparency = moved_trans[0]
    front_part = jnp.dot(response, nearer_radiance, precision=lax.Precision.HIGHEST)
    slab_portion = jnp.dot(response, nearer_transparency * light, precision=lax.Precision.HIGHEST)
    nearer_slab_rgb, slab_colour_rgb = lax.psum((front_part, slab_portion), "spec")
    image = lax.psum(slab_colour_rgb, "depth")
    return (nearer_slab_rgb[None], image)


def solution(mesh):
    placed = (
        P("depth", "spec", None),
        P("depth", "spec", None),
        P("spec"),
        P(),
        P(),
        P(None, "spec"),
    )
    return jax.shard_map(
        body, mesh=mesh, in_specs=placed, out_specs=(P("depth", None, None), P()), check_vma=False
    )
```

profile of v0, /device:TPU:0, one launch (start us, length us, event | category | flops | bytes accessed | tf_op | source)
XLA Modules:
  0.0 190.8 jit_solution(17573433646198136472)
XLA Ops:
  0.7 0.8 and_select_fusion
  1.5 5.9 %fusion = f32[32,2048]{1,0:T(8,128)S(1)} fusion(f32[32]{0:T(128)} %param.8, f32[32,2048]{1,0:T(8,128)S(1)} %and_select_fusion, bf16[32,32,2048]{2,1,0:T(8,128)(2,1)} %param.7), kind=kLoop, calls=%fused_computation.2 | loop fusion | flops 10420224 | bytes 4718720 | tf_op jit(solution)/shard_map/reduce_sum | solution.py:25
  7.4 0.6 copy.48
  8.0 0.5 broadcast.88
  8.5 9.3 %reduce = f32[2048,32]{1,0:T(8,128)S(1)} reduce(f32[2048,1,32]{2,1,0:T(1,128)S(1)} %bitcast.63, f32[]{:T(128)} %broadcast.88), dimensions={1}, to_apply=%bitcast.47.reduce_sub_computation | reduce | bytes 524292
  17.9 1.1 reshape.76
  19.0 8.3 %all-to-all-start.1 = ((f32[16,1,4096]{2,1,0:T(1,128)}), f32[16,1,4096]{2,1,0:T(1,128)S(1)}, u32[]{:S(2)}, u32[]{:S(2)}) async-start(f32[16,1,4096]{2,1,0:T(1,128)} %reshape.76), calls=%async_computation.1 | async-start | bytes 524288 | tf_op jit(solution)/shard_map/all_to_all | solution.py:28
  27.4 21.2 %multiply_reduce_fusion = f32[32,2048]{1,0:T(8,128)S(1)} fusion(bf16[32,32,2048]{2,1,0:T(8,128)(2,1)} %param.6, f32[32]{0:T(128)S(1)} %copy-done.1, f32[32,2048]{1,0:T(8,128)S(1)} %and_select_fusion, bf16[32,32,2048]{2,1,0:T(8,128)(2,1)} %param.7), kind=kOutput, calls=%fused_computation | convolution fusion | flops 826214400 | bytes 8913024 | tf_op jit(solution)/shard_map/ij,jbr->ibr/dot_general | solution.py:21
  48.6 0.6 copy.46
  49.2 9.6 %reduce.2 = f32[2048,32]{1,0:T(8,128)S(1)} reduce(f32[2048,1,32]{2,1,0:T(1,128)S(1)} %bitcast.66, f32[]{:T(128)} %broadcast.88), dimensions={1}, to_apply=%bitcast.45.reduce_sub_computation | reduce | bytes 524292
  58.8 1.2 reshape.74
  59.9 6.9 %all-to-all-start = ((f32[16,1,4096]{2,1,0:T(1,128)}), f32[16,1,4096]{2,1,0:T(1,128)S(1)}, u32[]{:S(2)}, u32[]{:S(2)}) async-start(f32[16,1,4096]{2,1,0:T(1,128)} %reshape.74), calls=%async_computation | async-start | bytes 524288 | tf_op jit(solution)/shard_map/all_to_all | solution.py:27
  66.8 1.3 reduce.1
  68.1 1.8 reshape.77
  69.9 0.6 copy.49
  70.9 5.3 %all-to-all-done = f32[16,1,4096]{2,1,0:T(1,128)S(1)} async-done(((f32[16,1,4096]{2,1,0:T(1,128)}), f32[16,1,4096]{2,1,0:T(1,128)S(1)}, u32[]{:S(2)}, u32[]{:S(2)}) %all-to-all-start) | async-done | bytes 262176 | tf_op jit(solution)/shard_map/all_to_all | solution.py:27
  76.2 1.3 reduce.3
  77.4 1.8 reshape.75
  79.3 0.3 copy.57
  80.7 0.1 slice.138
  80.8 0.1 slice.135
  80.9 0.1 slice.133
  81.0 0.1 slice.136
  81.5 0.4 pad.59
  81.9 0.4 pad.58
  82.4 0.4 pad.56
  82.8 0.4 pad.57
  83.4 0.2 pad.60
  83.7 0.2 pad.62
  83.9 0.2 pad.63
  84.1 0.2 pad.61
  84.5 0.2 pad.84
  84.8 0.2 pad.125
  85.2 0.7 concatenate.31.clone
  85.9 3.5 %all-to-all-start.3 = ((f32[16,32,128]{2,1,0:T(8,128)}), f32[16,32,128]{2,1,0:T(8,128)S(1)}, u32[]{:S(2)}, u32[]{:S(2)}) async-start(f32[16,32,128]{2,1,0:T(8,128)} %concatenate.31.clone), calls=%async_computation.3 | async-start | bytes 524288 | tf_op jit(solution)/shard_map/all_to_all | solution.py:34
  89.5 0.2 pad.82
  89.7 0.2 pad.124
  90.1 0.7 concatenate.29.clone
  90.8 7.8 %all-to-all-done.3 = f32[16,32,128]{2,1,0:T(8,128)S(1)} async-done(((f32[16,32,128]{2,1,0:T(8,128)}), f32[16,32,128]{2,1,0:T(8,128)S(1)}, u32[]{:S(2)}, u32[]{:S(2)}) %all-to-all-start.3) | async-done | bytes 262176 | tf_op jit(solution)/shard_map/all_to_all | solution.py:34
  98.7 3.5 %all-to-all-start.2 = ((f32[16,32,128]{2,1,0:T(8,128)}), f32[16,32,128]{2,1,0:T(8,128)S(1)}, u32[]{:S(2)}, u32[]{:S(2)}) async-start(f32[16,32,128]{2,1,0:T(8,128)} %concatenate.29.clone), calls=%async_computation.2 | async-start | bytes 524288 | tf_op jit(solution)/shard_map/all_to_all | solution.py:33
  102.2 0.2 copy.55
  102.4 9.0 %all-to-all-done.2 = f32[16,32,128]{2,1,0:T(8,128)S(1)} async-done(((f32[16,32,128]{2,1,0:T(8,128)}), f32[16,32,128]{2,1,0:T(8,128)S(1)}, u32[]{:S(2)}, u32[]{:S(2)}) %all-to-all-start.2) | async-done | bytes 262176 | tf_op jit(solution)/shard_map/all_to_all | solution.py:33
  111.4 0.2 copy.52
  111.5 0.3 convolution_bitcast_fusion
  111.9 0.3 convolution_bitcast_fusion.1
  112.2 3.6 %all-reduce.18 = (f32[1,3,2048]{2,1,0:T(4,128)S(1)}, f32[3,2048]{1,0:T(4,128)S(1)}) all-reduce(f32[1,3,2048]{2,1,0:T(4,128)S(1)} %convolution_bitcast_fusion.1, f32[3,2048]{1,0:T(4,128)S(1)} %convolution_bitcast_fusion), channel_id=1, replica_groups=mesh['depth'=16,'spec'=2] {'spec'}, use_global_device_ids=true, to_apply=%region_2.3 | all-reduce | flops 12288 | bytes 98304 | tf_op jit(solution)/shard_map/psum | solution.py:39
  115.8 0.6 copy.56
  116.5 74.4 %psum.23 = f32[3,2048]{1,0:T(4,128)} all-reduce(f32[3,2048]{1,0:T(4,128)S(1)} %get-tuple-element.13), channel_id=1, replica_groups=mesh['depth'=16,'spec'=2] {'depth'}, use_global_device_ids=true, to_apply=%region_4.5 | all-reduce | flops 6144 | bytes 49152 | tf_op jit(solution)/shard_map/psum | solution.py:40
  (45 shorter events, 2.2 us)
Async XLA Ops:
  0.6 110.9 %copy-start = (f32[3,32]{1,0:T(4,128)S(1)}, f32[3,32]{1,0:T(4,128)}, u32[]{:S(2)}) copy-start(f32[3,32]{1,0:T(4,128)} %param.11) | copy-start | bytes 1156
  1.5 25.9 %copy-start.1 = (f32[32]{0:T(128)S(1)}, f32[32]{0:T(128)}, u32[]{:S(2)}) copy-start(f32[32]{0:T(128)} %param.8) | copy-start | bytes 388
  19.0 40.9 %all-to-all-start.1 = ((f32[16,1,4096]{2,1,0:T(1,128)}), f32[16,1,4096]{2,1,0:T(1,128)S(1)}, u32[]{:S(2)}, u32[]{:S(2)}) async-start(f32[16,1,4096]{2,1,0:T(1,128)} %reshape.76), calls=%async_computation.1 | async-start | bytes 524288 | tf_op jit(solution)/shard_map/all_to_all | solution.py:28
  59.9 16.2 %all-to-all-start = ((f32[16,1,4096]{2,1,0:T(1,128)}), f32[16,1,4096]{2,1,0:T(1,128)S(1)}, u32[]{:S(2)}, u32[]{:S(2)}) async-start(f32[16,1,4096]{2,1,0:T(1,128)} %reshape.74), calls=%async_computation | async-start | bytes 524288 | tf_op jit(solution)/shard_map/all_to_all | solution.py:27
  85.9 12.8 %all-to-all-start.3 = ((f32[16,32,128]{2,1,0:T(8,128)}), f32[16,32,128]{2,1,0:T(8,128)S(1)}, u32[]{:S(2)}, u32[]{:S(2)}) async-start(f32[16,32,128]{2,1,0:T(8,128)} %concatenate.31.clone), calls=%async_computation.3 | async-start | bytes 524288 | tf_op jit(solution)/shard_map/all_to_all | solution.py:34
  98.7 12.7 %all-to-all-start.2 = ((f32[16,32,128]{2,1,0:T(8,128)}), f32[16,32,128]{2,1,0:T(8,128)S(1)}, u32[]{:S(2)}, u32[]{:S(2)}) async-start(f32[16,32,128]{2,1,0:T(8,128)} %concatenate.29.clone), calls=%async_computation.2 | async-start | bytes 524288 | tf_op jit(solution)/shard_map/all_to_all | solution.py:33
where the time goes:
time: 192 us; the launch traced here: 191 us
  blocking collectives  78 us (41%)
  other arithmetic  28.9 us (15%)
  starting transfers between devices  22.3 us (12%)
  waiting for transfers between devices  22.1 us (12%)
  matrix products  21.8 us (11%)
  local copies, waits for them, and re-layouts  16.5 us (9%)
    psum x1, blocking collectives, body(): image = lax.psum(slab_colour_rgb, 'depth')  74.4 us
    dot_general x1, matrix products, body(): jnp.einsum('ij,jbr->ibr', lower, tau, precision=lax.Precision.HIGHEST)  21.2 us
    unnamed x2, other arithmetic  18.9 us
    all_to_all x1, waiting for transfers between devices, body(): lax.all_to_all(lead_light, 'depth', split_axis=0, concat_axis=2, tiled=True)  8.99 us
    all_to_all x1, starting transfers between devices, body(): lax.all_to_all(trans[None], 'depth', split_axis=2, concat_axis=0, tiled=T...  8.35 us
    all_to_all x1, waiting for transfers between devices, body(): lax.all_to_all(lead_trans, 'depth', split_axis=0, concat_axis=2, tiled=True)  7.84 us
    unnamed x14, local copies, waits for them, and re-layouts  7.74 us
    all_to_all x1, starting transfers between devices, body(): lax.all_to_all(light[None], 'depth', split_axis=2, concat_axis=0, tiled=T...  6.9 us
  transfers between devices with their start and end apart: 4, of which 3 were waited for; matrix products, arithmetic and copies ran while one was open for 20% of the time, Pallas kernels for 0%

commit v1 on v0

--- a/solution.py
+++ b/solution.py
@@ -2,6 +2,13 @@
 import jax.numpy as jnp
 from jax import lax
 from jax.sharding import PartitionSpec as P
+
+
+def swap_blocks(x, name, split, join):
+    count = lax.axis_size(name)
+    shards = jnp.stack(jnp.split(x, count, axis=split), axis=0)
+    shards = lax.all_to_all(shards, name, split_axis=0, concat_axis=0)
+    return jnp.concatenate(shards, axis=join)
 
 
 def merge_slabs(earlier, later):
@@ -31,7 +38,7 @@
     lead_light = jnp.concatenate([jnp.zeros_like(pieces[0][:1]), totals[0][:-1]], axis=0)
     lead_trans = jnp.concatenate([jnp.ones_like(pieces[1][:1]), totals[1][:-1]], axis=0)
     moved_light = lax.all_to_all(lead_light, "depth", split_axis=0, concat_axis=2, tiled=True)
-    moved_trans = lax.all_to_all(lead_trans, "depth", split_axis=0, concat_axis=2, tiled=True)
+    moved_trans = swap_blocks(lead_trans, "depth", 0, 2)
     nearer_radiance = moved_light[0]
     nearer_transparency = moved_trans[0]
     front_part = jnp.dot(response, nearer_radiance, precision=lax.Precision.HIGHEST)

time: 192 us -> 202 us (1.052)
  local copies, waits for them, and re-layouts: 16.5 us -> 25.7 us
    unnamed x14 -> x29, local copies, waits for them, and re-layouts: 7.74 us -> 16.9 us
    all_to_all x1, waiting for transfers between devices: 5.3 us -> 0.01 us  [body(): lax.all_to_all(light[None], 'depth', split_axis=2, concat_axis=0, tiled=T...]
    all_to_all x1, waiting for transfers between devices: 0.01 us -> 5.06 us  [body(): lax.all_to_all(trans[None], 'depth', split_axis=2, concat_axis=0, tiled=T...]
  transfers between devices with their start and end apart: 4 -> 4, of which waited for: 3 -> 3; matrix products, arithmetic and copies ran while one was open for 20% -> 11% of each run, Pallas kernels for 0% -> 0%
where the time goes in v1:
time: 202 us; the launch traced here: 201 us
  blocking collectives  78 us (39%)
  other arithmetic  29.1 us (14%)
  local copies, waits for them, and re-layouts  25.7 us (13%)
  matrix products  22.6 us (11%)
  starting transfers between devices  22.4 us (11%)
  waiting for transfers between devices  21.9 us (11%)
    psum x1, blocking collectives, body(): image = lax.psum(slab_colour_rgb, 'depth')  74.4 us
    dot_general x1, matrix products, body(): jnp.einsum('ij,jbr->ibr', lower, tau, precision=lax.Precision.HIGHEST)  21.9 us
    unnamed x2, other arithmetic  18.9 us
    unnamed x29, local copies, waits for them, and re-layouts  16.9 us
    all_to_all x1, waiting for transfers between devices, body(): lax.all_to_all(lead_light, 'depth', split_axis=0, concat_axis=2, tiled=True)  8.98 us
    all_to_all x1, starting transfers between devices, body(): lax.all_to_all(light[None], 'depth', split_axis=2, concat_axis=0, tiled=T...  8.34 us
    all_to_all x1, waiting for transfers between devices, swap_blocks(): shards = lax.all_to_all(shards, name, split_axis=0, concat_axis=0)  7.82 us
    all_to_all x1, starting transfers between devices, body(): lax.all_to_all(trans[None], 'depth', split_axis=2, concat_axis=0, tiled=T...  6.91 us
  transfers between devices with their start and end apart: 4, of which 3 were waited for; matrix products, arithmetic and copies ran while one was open for 11% of the time, Pallas kernels for 0%

profile of v1, /device:TPU:0, one launch (start us, length us, event | category | flops | bytes accessed | tf_op | source)
XLA Modules:
  0.0 200.9 jit_solution(1493234309250570717)
XLA Ops:
  0.7 0.8 and_select_fusion
  1.5 21.9 %multiply_reduce_fusion = f32[32,2048]{1,0:T(8,128)S(1)} fusion(bf16[32,32,2048]{2,1,0:T(8,128)(2,1)} %param.6, f32[32]{0:T(128)} %param.8, f32[32,2048]{1,0:T(8,128)S(1)} %and_select_fusion, bf16[32,32,2048]{2,1,0:T(8,128)(2,1)} %param.7), kind=kOutput, calls=%fused_computation | convolution fusion | flops 826214400 | bytes 8913024 | tf_op jit(solution)/shard_map/ij,jbr->ibr/dot_general | solution.py:28
  23.4 0.6 copy.118
  24.0 0.5 broadcast.86
  24.6 9.5 %reduce.2 = f32[2048,32]{1,0:T(8,128)S(1)} reduce(f32[2048,1,32]{2,1,0:T(1,128)S(1)} %bitcast.104, f32[]{:T(128)} %broadcast.86), dimensions={1}, to_apply=%bitcast.86.reduce_sub_computation | reduce | bytes 524292
  34.1 1.2 reshape.77
  35.2 8.3 %all-to-all-start = ((f32[16,1,4096]{2,1,0:T(1,128)}), f32[16,1,4096]{2,1,0:T(1,128)S(1)}, u32[]{:S(2)}, u32[]{:S(2)}) async-start(f32[16,1,4096]{2,1,0:T(1,128)} %reshape.77), calls=%async_computation | async-start | bytes 524288 | tf_op jit(solution)/shard_map/all_to_all | solution.py:34
  43.6 5.9 %fusion = f32[32,2048]{1,0:T(8,128)S(1)} fusion(f32[32]{0:T(128)S(1)} %copy-done.1, f32[32,2048]{1,0:T(8,128)S(1)} %and_select_fusion, bf16[32,32,2048]{2,1,0:T(8,128)(2,1)} %param.7), kind=kLoop, calls=%fused_computation.2 | loop fusion | flops 10420224 | bytes 4718720 | tf_op jit(solution)/shard_map/reduce_sum | solution.py:32
  49.5 0.6 copy.120
  50.1 9.3 %reduce = f32[2048,32]{1,0:T(8,128)S(1)} reduce(f32[2048,1,32]{2,1,0:T(1,128)S(1)} %bitcast.105, f32[]{:T(128)} %broadcast.86), dimensions={1}, to_apply=%bitcast.88.reduce_sub_computation | reduce | bytes 524292
  59.5 1.1 reshape.79
  60.6 6.9 %all-to-all-start.1 = ((f32[16,1,4096]{2,1,0:T(1,128)}), f32[16,1,4096]{2,1,0:T(1,128)S(1)}, u32[]{:S(2)}, u32[]{:S(2)}) async-start(f32[16,1,4096]{2,1,0:T(1,128)} %reshape.79), calls=%async_computation.1 | async-start | bytes 524288 | tf_op jit(solution)/shard_map/all_to_all | solution.py:35
  67.5 0.6 constant_dynamic-update-slice_fusion.15
  68.1 1.3 reduce.3
  69.4 1.8 reshape.78
  71.2 0.3 copy.142
  71.8 5.1 %all-to-all-done.1 = f32[16,1,4096]{2,1,0:T(1,128)S(1)} async-done(((f32[16,1,4096]{2,1,0:T(1,128)}), f32[16,1,4096]{2,1,0:T(1,128)S(1)}, u32[]{:S(2)}, u32[]{:S(2)}) %all-to-all-start.1) | async-done | bytes 262176 | tf_op jit(solution)/shard_map/all_to_all | solution.py:35
  76.8 1.3 reduce.1
  78.1 1.8 reshape.80
  79.9 0.6 copy.121
  82.5 0.4 pad.55
  83.0 0.4 pad.56
  83.4 0.4 pad.58
  83.8 0.4 pad.57
  86.9 0.6 constant_dynamic-update-slice_fusion.14
  87.5 0.6 constant_dynamic-update-slice_fusion.13
  88.1 0.6 constant_dynamic-update-slice_fusion.12
  88.7 0.6 constant_dynamic-update-slice_fusion.11
  89.3 0.6 constant_dynamic-update-slice_fusion.10
  89.9 0.6 constant_dynamic-update-slice_fusion.9
  90.5 0.6 constant_dynamic-update-slice_fusion.8
  91.1 0.6 constant_dynamic-update-slice_fusion.7
  91.7 0.6 constant_dynamic-update-slice_fusion.6
  92.3 0.6 constant_dynamic-update-slice_fusion.5
  92.9 0.6 constant_dynamic-update-slice_fusion.4
  93.5 0.6 constant_dynamic-update-slice_fusion.3
  94.1 0.6 constant_dynamic-update-slice_fusion.2
  94.7 0.6 constant_dynamic-update-slice_fusion.1
  95.3 0.6 constant_dynamic-update-slice_fusion
  95.9 3.5 %all-to-all-start.3 = ((f32[16,1,32,128]{3,2,1,0:T(8,128)}), f32[16,1,32,128]{3,2,1,0:T(8,128)S(1)}, u32[]{:S(2)}, u32[]{:S(2)}) async-start(f32[16,1,32,128]{3,2,1,0:T(8,128)} %constant_dynamic-update-slice_fusion), calls=%async_computation.3 | async-start | bytes 524288 | tf_op jit(solution)/shard_map/all_to_all | solution.py:10
  100.2 0.7 concatenate.26.clone
  100.9 7.8 %all-to-all-done.3 = f32[16,1,32,128]{3,2,1,0:T(8,128)S(1)} async-done(((f32[16,1,32,128]{3,2,1,0:T(8,128)}), f32[16,1,32,128]{3,2,1,0:T(8,128)S(1)}, u32[]{:S(2)}, u32[]{:S(2)}) %all-to-all-start.3) | async-done | bytes 262176 | tf_op jit(solution)/shard_map/all_to_all | solution.py:10
  108.7 3.5 %all-to-all-start.2 = ((f32[16,32,128]{2,1,0:T(8,128)}), f32[16,32,128]{2,1,0:T(8,128)S(1)}, u32[]{:S(2)}, u32[]{:S(2)}) async-start(f32[16,32,128]{2,1,0:T(8,128)} %concatenate.26.clone), calls=%async_computation.2 | async-start | bytes 524288 | tf_op jit(solution)/shard_map/all_to_all | solution.py:40
  112.4 9.0 %all-to-all-done.2 = f32[16,32,128]{2,1,0:T(8,128)S(1)} async-done(((f32[16,32,128]{2,1,0:T(8,128)}), f32[16,32,128]{2,1,0:T(8,128)S(1)}, u32[]{:S(2)}, u32[]{:S(2)}) %all-to-all-start.2) | async-done | bytes 262176 | tf_op jit(solution)/shard_map/all_to_all | solution.py:40
  121.6 0.3 convolution_bitcast_fusion
  122.2 3.6 %all-reduce.17 = (f32[1,3,2048]{2,1,0:T(4,128)S(1)}, f32[3,2048]{1,0:T(4,128)S(1)}) all-reduce(f32[1,3,2048]{2,1,0:T(4,128)S(1)} %convolution_bitcast_fusion.1, f32[3,2048]{1,0:T(4,128)S(1)} %convolution_bitcast_fusion), channel_id=1, replica_groups=mesh['depth'=16,'spec'=2] {'spec'}, use_global_device_ids=true, to_apply=%region_2.3 | all-reduce | flops 12288 | bytes 98304 | tf_op jit(solution)/shard_map/psum | solution.py:46
  125.9 74.4 %psum.23 = f32[3,2048]{1,0:T(4,128)} all-reduce(f32[3,2048]{1,0:T(4,128)S(1)} %get-tuple-element.15), channel_id=1, replica_groups=mesh['depth'=16,'spec'=2] {'depth'}, use_global_device_ids=true, to_apply=%region_4.5 | all-reduce | flops 6144 | bytes 49152 | tf_op jit(solution)/shard_map/psum | solution.py:47
  200.2 0.6 copy.141
  (63 shorter events, 5.9 us)
Async XLA Ops:
  0.6 120.9 %copy-start = (f32[3,32]{1,0:T(4,128)S(1)}, f32[3,32]{1,0:T(4,128)}, u32[]{:S(2)}) copy-start(f32[3,32]{1,0:T(4,128)} %param.11) | copy-start | bytes 1156
  23.4 20.2 %copy-start.1 = (f32[32]{0:T(128)S(1)}, f32[32]{0:T(128)}, u32[]{:S(2)}) copy-start(f32[32]{0:T(128)} %param.8) | copy-start | bytes 388
  35.2 25.4 %all-to-all-start = ((f32[16,1,4096]{2,1,0:T(1,128)}), f32[16,1,4096]{2,1,0:T(1,128)S(1)}, u32[]{:S(2)}, u32[]{:S(2)}) async-start(f32[16,1,4096]{2,1,0:T(1,128)} %reshape.77), calls=%async_computation | async-start | bytes 524288 | tf_op jit(solution)/shard_map/all_to_all | solution.py:34
  60.6 16.2 %all-to-all-start.1 = ((f32[16,1,4096]{2,1,0:T(1,128)}), f32[16,1,4096]{2,1,0:T(1,128)S(1)}, u32[]{:S(2)}, u32[]{:S(2)}) async-start(f32[16,1,4096]{2,1,0:T(1,128)} %reshape.79), calls=%async_computation.1 | async-start | bytes 524288 | tf_op jit(solution)/shard_map/all_to_all | solution.py:35
  95.9 12.8 %all-to-all-start.3 = ((f32[16,1,32,128]{3,2,1,0:T(8,128)}), f32[16,1,32,128]{3,2,1,0:T(8,128)S(1)}, u32[]{:S(2)}, u32[]{:S(2)}) async-start(f32[16,1,32,128]{3,2,1,0:T(8,128)} %constant_dynamic-update-slice_fusion), calls=%async_computation.3 | async-start | bytes 524288 | tf_op jit(solution)/shard_map/all_to_all | solution.py:10
  108.7 12.7 %all-to-all-start.2 = ((f32[16,32,128]{2,1,0:T(8,128)}), f32[16,32,128]{2,1,0:T(8,128)S(1)}, u32[]{:S(2)}, u32[]{:S(2)}) async-start(f32[16,32,128]{2,1,0:T(8,128)} %concatenate.26.clone), calls=%async_computation.2 | async-start | bytes 524288 | tf_op jit(solution)/shard_map/all_to_all | solution.py:40
